TPU v7x, 8 devices: a whole 2x2x1 slice. The times are simulated.
8 devices in a mesh: dp: 1 (over z), sp: 8 (over y, x, core).
Axes of the slice: x: 2, y: 2, z: 1, core: 2. Of those that a mesh axis runs over, the one named last changes fastest.
Arguments:
- hidden: bfloat16 [6144, 5120], P(('dp', 'sp'))
- pos_ids: int32 [3, 6144], P(None, ('dp', 'sp'))
- cu_doc: int32 [3], P('dp')
- grad_y: bfloat16 [6144, 5120], P(('dp', 'sp'))
- norm_w: bfloat16 [5120], replicated
- w_q: bfloat16 [5120, 5120], replicated
- b_q: bfloat16 [5120], replicated
- w_k: bfloat16 [5120, 1024], replicated
- b_k: bfloat16 [1024], replicated
- w_v: bfloat16 [5120, 1024], replicated
- b_v: bfloat16 [1024], replicated
- w_o: bfloat16 [5120, 5120], replicated
Outputs:
- output 1: bfloat16 [6144, 5120], P(('dp', 'sp'))
- output 2: bfloat16 [6144, 5120], P(('dp', 'sp'))
- output 3: float32 [5120], P(('dp', 'sp'))
- output 4: float32 [5120, 5120], P(('dp', 'sp'))
- output 5: float32 [5120], P(('dp', 'sp'))
- output 6: float32 [5120, 1024], P(('dp', 'sp'))
- output 7: float32 [1024], P(('dp', 'sp'))
- output 8: float32 [5120, 1024], P(('dp', 'sp'))
- output 9: float32 [1024], P(('dp', 'sp'))
- output 10: float32 [5120, 5120], P(('dp', 'sp'))
All inputs are finite; a program needn't handle non-finite values.
Results may differ from a plain program's by a relative error of at most 0.015078.
Values are sent between devices in bfloat16 or wider.
A program may use at most 1 GiB of HBM per device.

v0:
```python
import math
import jax
import jax.numpy as jnp
from jax import lax
from jax.sharding import PartitionSpec as P

HEAD_DIM = 128
SECTION_ONE = 16
SECTION_TWO = 40
ROW_BUDGET = 512
ROPE_BASE = 1000000.0
NORM_EPS = 1e-6


def rope_tables(pos_ids):
    freq_idx = jnp.arange(HEAD_DIM // 2)
    inv_freq = 1.0 / jnp.power(ROPE_BASE, jnp.arange(0, HEAD_DIM, 2).astype(jnp.float32) / HEAD_DIM)
    pos_f = pos_ids.astype(jnp.float32)
    chosen = jnp.where(freq_idx[None, :] < SECTION_ONE, pos_f[0][:, None], jnp.where(freq_idx[None, :] < SECTION_TWO, pos_f[1][:, None], pos_f[2][:, None]))
    angles = chosen * inv_freq[None, :]
    angles = jnp.concatenate([angles, angles], axis=-1)
    return jnp.cos(angles), jnp.sin(angles)


def rotate(values, cos_t, sin_t):
    half_dim = values.shape[-1] // 2
    turned = jnp.concatenate([-values[..., half_dim:], values[..., :half_dim]], axis=-1)
    return values * cos_t[:, None, :] + turned * sin_t[:, None, :]


def unrotate(grad_in, cos_t, sin_t):
    half_dim = grad_in.shape[-1] // 2
    scaled = grad_in * sin_t[:, None, :]
    turned = jnp.concatenate([scaled[..., half_dim:], -scaled[..., :half_dim]], axis=-1)
    return grad_in * cos_t[:, None, :] + turned


def doc_starts(cu_doc, tok_idx):
    bounds = cu_doc[:-1]
    return jnp.max(jnp.where(bounds[None, :] <= tok_idx[:, None], bounds[None, :], 0), axis=1)


def attend(q_grp, k_all, v_all, do_grp, q_first, starts):
    n_query, groups, grp_ratio, head_dim = q_grp.shape
    key_len = k_all.shape[0]
    row_cap = max(1, ROW_BUDGET // (groups * grp_ratio))
    block_len = math.gcd(n_query, 1 << (row_cap.bit_length() - 1))
    n_blocks = n_query // block_len
    qk_scale = 1.0 / math.sqrt(head_dim)
    key_idx = jnp.arange(key_len)

    def block_step(acc_pair, block_in):
        dk_acc, dv_acc = acc_pair
        q_blk, do_blk, start_blk, blk_idx = block_in
        q_idx = q_first + blk_idx * block_len + jnp.arange(block_len)
        allowed = (key_idx[None, :] <= q_idx[:, None]) & (key_idx[None, :] >= start_blk[:, None])
        scores = jnp.einsum("qgre,kge->gqrk", q_blk, k_all, preferred_element_type=jnp.float32) * qk_scale
        scores = jnp.where(allowed[None, :, None, :], scores, -1e30)
        prob_f = jax.nn.softmax(scores, axis=-1)
        prob_b = prob_f.astype(jnp.bfloat16)
        out_blk = jnp.einsum("gqrk,kge->qgre", prob_b, v_all, preferred_element_type=jnp.float32).astype(jnp.bfloat16)
        d_prob = jnp.einsum("qgre,kge->gqrk", do_blk, v_all, preferred_element_type=jnp.float32)
        row_delta = jnp.sum(prob_f * d_prob, axis=-1, keepdims=True)
        d_score = (prob_f * (d_prob - row_delta) * qk_scale).astype(jnp.bfloat16)
        dq_blk = jnp.einsum("gqrk,kge->qgre", d_score, k_all, preferred_element_type=jnp.float32).astype(jnp.bfloat16)
        dk_acc = dk_acc + jnp.einsum("gqrk,qgre->kge", d_score, q_blk, preferred_element_type=jnp.float32)
        dv_acc = dv_acc + jnp.einsum("gqrk,qgre->kge", prob_b, do_blk, preferred_element_type=jnp.float32)
        return (dk_acc, dv_acc), (out_blk, dq_blk)

    blocks_in = (q_grp.reshape(n_blocks, block_len, groups, grp_ratio, head_dim), do_grp.reshape(n_blocks, block_len, groups, grp_ratio, head_dim), starts.reshape(n_blocks, block_len), jnp.arange(n_blocks))
    zero_acc = jnp.zeros((key_len, groups, head_dim), jnp.float32)
    acc_pair, outs_pair = lax.scan(block_step, (zero_acc, zero_acc), blocks_in)
    return outs_pair[0].reshape(q_grp.shape), outs_pair[1].reshape(q_grp.shape), acc_pair[0], acc_pair[1]


def front(hidden, pos_ids, grad_y, norm_w, w_q, b_q, w_k, b_k, w_v, b_v, w_o):
    tokens = hidden.shape[0]
    num_heads = w_q.shape[1] // HEAD_DIM
    num_kv = w_k.shape[1] // HEAD_DIM
    h_f32 = hidden.astype(jnp.float32)
    inv_rms = lax.rsqrt(jnp.mean(h_f32 * h_f32, axis=-1, keepdims=True) + NORM_EPS)
    normed = h_f32 * inv_rms
    normed_b = (normed * norm_w.astype(jnp.float32)).astype(jnp.bfloat16)
    cos_t, sin_t = rope_tables(pos_ids)
    q_lin = jnp.dot(normed_b, w_q, preferred_element_type=jnp.float32) + b_q.astype(jnp.float32)
    k_lin = jnp.dot(normed_b, w_k, preferred_element_type=jnp.float32) + b_k.astype(jnp.float32)
    q_rot = rotate(q_lin.reshape(tokens, num_heads, HEAD_DIM), cos_t, sin_t).astype(jnp.bfloat16)
    k_rot = rotate(k_lin.reshape(tokens, num_kv, HEAD_DIM), cos_t, sin_t).astype(jnp.bfloat16)
    v_val = (jnp.dot(normed_b, w_v, preferred_element_type=jnp.float32) + b_v.astype(jnp.float32)).astype(jnp.bfloat16).reshape(tokens, num_kv, HEAD_DIM)
    d_attn = jnp.einsum("td,qd->tq", grad_y, w_o, preferred_element_type=jnp.float32).astype(jnp.bfloat16).reshape(tokens, num_heads, HEAD_DIM)
    saved = (h_f32, inv_rms, normed, normed_b, cos_t, sin_t)
    return saved, q_rot, k_rot, v_val, d_attn


def finish(saved, attn_out, dq_rot, dk_rot, dv_val, grad_y, norm_w, w_q, w_k, w_v, w_o):
    h_f32, inv_rms, normed, normed_b, cos_t, sin_t = saved
    tokens = h_f32.shape[0]
    attn_flat = attn_out.reshape(tokens, -1)
    y_out = (h_f32 + jnp.dot(attn_flat, w_o, preferred_element_type=jnp.float32)).astype(jnp.bfloat16)
    grad_w_o = jnp.einsum("tq,td->qd", attn_flat, grad_y, preferred_element_type=jnp.float32)
    dq_lin = unrotate(dq_rot.astype(jnp.float32), cos_t, sin_t).reshape(tokens, -1)
    dk_lin = unrotate(dk_rot.astype(jnp.float32), cos_t, sin_t).reshape(tokens, -1)
    dv_lin = dv_val.reshape(tokens, -1)
    dq_b = dq_lin.astype(jnp.bfloat16)
    dk_b = dk_lin.astype(jnp.bfloat16)
    grad_b_q = jnp.sum(dq_lin, axis=0)
    grad_b_k = jnp.sum(dk_lin, axis=0)
    grad_b_v = jnp.sum(dv_lin.astype(jnp.float32), axis=0)
    grad_w_q = jnp.einsum("td,tq->dq", normed_b, dq_b, preferred_element_type=jnp.float32)
    grad_w_k = jnp.einsum("td,tq->dq", normed_b, dk_b, preferred_element_type=jnp.float32)
    grad_w_v = jnp.einsum("td,tq->dq", normed_b, dv_lin, preferred_element_type=jnp.float32)
    d_norm = jnp.einsum("tq,dq->td", dq_b, w_q, preferred_element_type=jnp.float32) + jnp.einsum("tq,dq->td", dk_b, w_k, preferred_element_type=jnp.float32) + jnp.einsum("tq,dq->td", dv_lin, w_v, preferred_element_type=jnp.float32)
    grad_norm_w = jnp.sum(d_norm * normed, axis=0)
    d_scaled = d_norm * norm_w.astype(jnp.float32)
    d_hidden = inv_rms * (d_scaled - normed * jnp.mean(d_scaled * normed, axis=-1, keepdims=True))
    grad_hidden = (grad_y.astype(jnp.float32) + d_hidden).astype(jnp.bfloat16)
    return (y_out, grad_hidden, grad_norm_w, grad_w_q, grad_b_q, grad_w_k, grad_b_k, grad_w_v, grad_b_v, grad_w_o)


def solution(mesh):
    group_devs = mesh.shape["sp"]
    tok_spec = P(("dp", "sp"), None)
    vec_spec = P(("dp", "sp"))
    rep_spec = P()

    def per_device(hidden, pos_ids, cu_doc, grad_y, norm_w, w_q, b_q, w_k, b_k, w_v, b_v, w_o):
        tokens = hidden.shape[0]
        seq_len = tokens * group_devs
        saved, q_rot, k_rot, v_val, d_attn = front(hidden, pos_ids, grad_y, norm_w, w_q, b_q, w_k, b_k, w_v, b_v, w_o)
        q_heads = lax.all_to_all(q_rot, "sp", 1, 0, tiled=True)
        k_heads = lax.all_to_all(k_rot, "sp", 1, 0, tiled=True)
        v_heads = lax.all_to_all(v_val, "sp", 1, 0, tiled=True)
        do_heads = lax.all_to_all(d_attn, "sp", 1, 0, tiled=True)
        loc_heads = q_heads.shape[1]
        loc_kv = k_heads.shape[1]
        starts = doc_starts(cu_doc, jnp.arange(seq_len))
        out_h, dq_h, dk_h, dv_h = attend(q_heads.reshape(seq_len, loc_kv, loc_heads // loc_kv, HEAD_DIM), k_heads, v_heads, do_heads.reshape(seq_len, loc_kv, loc_heads // loc_kv, HEAD_DIM), 0, starts)
        attn_out = lax.all_to_all(out_h.reshape(seq_len, loc_heads, HEAD_DIM), "sp", 0, 1, tiled=True)
        dq_rot = lax.all_to_all(dq_h.reshape(seq_len, loc_heads, HEAD_DIM), "sp", 0, 1, tiled=True)
        dk_rot = lax.all_to_all(dk_h.astype(jnp.bfloat16), "sp", 0, 1, tiled=True)
        dv_val = lax.all_to_all(dv_h.astype(jnp.bfloat16), "sp", 0, 1, tiled=True)
        results = finish(saved, attn_out, dq_rot, dk_rot, dv_val, grad_y, norm_w, w_q, w_k, w_v, w_o)
        summed = tuple(lax.psum_scatter(grad_part, "sp", scatter_dimension=0, tiled=True) for grad_part in results[2:])
        return (results[0], results[1]) + summed

    in_specs = (tok_spec, P(None, ("dp", "sp")), P("dp"), tok_spec, rep_spec, rep_spec, rep_spec, rep_spec, rep_spec, rep_spec, rep_spec, rep_spec)
    out_specs = (tok_spec, tok_spec, vec_spec, tok_spec, vec_spec, tok_spec, vec_spec, tok_spec, vec_spec, tok_spec)
    return jax.shard_map(per_device, mesh=mesh, in_specs=in_specs, out_specs=out_specs, check_vma=False)
```

profile of v0, /device:TPU:0, one launch (start us, length us, event | category | flops | bytes accessed | tf_op | source)
XLA Modules:
  0.0 5633.5 jit_solution(11171001469042525661)
XLA Ops:
  30.5 49.1 fusion.80
  93.2 49.8 add_bitcast_fusion
  158.2 24.7 slice_negate_fusion.1
  217.1 72.3 %all-to-all-done = bf16[768,40,128]{2,0,1:T(8,128)(2,1)} async-done(((bf16[768,40,128]{2,0,1:T(8,128)(2,1)}), bf16[768,40,128]{2,0,1:T(8,128)(2,1)}, u32[]{:S(2)}, u32[]{:S(2)}) %all-to-all-start) | async-done | bytes 7864352 | tf_op jit(solution)/shard_map/all_to_all | solution.py:130
  312.6 3684.2 %while.18 = (s32[]{:T(128)}, f32[6144,1,128]{0,2,1:T(8,128)}, f32[6144,1,128]{0,2,1:T(8,128)}, bf16[96,64,1,5,128]{4,1,0,3,2:T(8,128)(2,1)}, bf16[96,64,1,5,128]...) while((s32[]{:T(128)}, f32[6144,1,128]{0,2,1:T(8,128)}, ...), condition=%wide.region_6.7_spmd.clone.clone, body=%wide.region_2.6_spmd.clone.clone.sunk | while | flops 3053810176 | bytes 167221824 | solution.py:72
  329.4 14.3 fusion.174
  366.8 14.3 fusion.174
  405.2 14.3 fusion.174
  443.5 14.3 fusion.174
  481.9 14.3 fusion.174
  520.3 14.3 fusion.174
  558.7 14.3 fusion.174
  597.1 14.3 fusion.174
  635.5 14.3 fusion.174
  673.8 14.3 fusion.174
  712.2 14.3 fusion.174
  750.6 14.3 fusion.174
  789.0 14.3 fusion.174
  827.4 14.3 fusion.174
  865.8 14.3 fusion.174
  904.1 14.3 fusion.174
  942.5 14.3 fusion.174
  980.9 14.3 fusion.174
  1019.3 14.3 fusion.174
  1364.7 14.3 fusion.174
  1710.2 14.3 fusion.174
  2823.3 14.3 fusion.174
  3168.8 14.3 fusion.174
  4002.7 22.3 all_to_all.114
  4031.8 17.8 fusion.92
  4062.1 19.9 all-to-all-done.6
  4105.2 17.5 fusion.94
  4131.7 196.8 %all_to_all.115 = bf16[6144,5,128]{2,1,0:T(8,128)(2,1)} all-to-all(bf16[6144,5,128]{2,1,0:T(8,128)(2,1)S(1)} %copy.184), channel_id=1, replica_groups=mesh['dp'=1,'sp'=8] {'sp'}, dimensions={0} | all-to-all | bytes 15728640 | tf_op jit(solution)/shard_map/all_to_all | solution.py:139
  4360.9 15.7 copy.186
  4394.4 16.1 pad_maximum_fusion
  4410.5 15.7 copy.189
  4440.3 53.1 fusion.96
  4502.4 171.9 %all_to_all.116 = bf16[6144,5,128]{2,1,0:T(8,128)(2,1)} all-to-all(bf16[6144,5,128]{2,1,0:T(8,128)(2,1)S(1)} %copy.180), channel_id=1, replica_groups=mesh['dp'=1,'sp'=8] {'sp'}, dimensions={0} | all-to-all | bytes 15728640 | tf_op jit(solution)/shard_map/all_to_all | solution.py:138
  4674.3 14.9 copy.182
  4689.2 52.7 fusion.106
  4743.8 15.8 fusion.105
  4769.9 49.7 fusion.104
  4819.6 25.5 fusion.74
  4845.1 23.6 all-reduce.6
  4871.2 14.4 fusion.73
  4885.7 49.9 fusion.76
  4935.6 138.1 %reduce-scatter.13.cloned.1.call-done = f32[640,5120]{1,0:T(8,128)} async-done(((f32[5120,5120]{1,0:T(8,128)}), f32[640,5120]{1,0:T(8,128)}) %reduce-scatter.13.cloned.1.call-update) | async-done | bytes 13107216
  5073.6 552.9 %reduce-scatter.15.cloned.1.call-done = f32[640,5120]{1,0:T(8,128)} async-done(((f32[5120,5120]{1,0:T(8,128)}), f32[640,5120]{1,0:T(8,128)}) %reduce-scatter.15.cloned.1.call-update) | async-done | bytes 13107216
  (2064 shorter events, 3542.5 us)
Async XLA Ops:
  13.0 188.0 %copy-start.26 = (f32[768]{0:T(1024)}, f32[768]{0:T(1024)S(1)}, u32[]{:S(2)}) copy-start(f32[768]{0:T(1024)S(1)} %add_rsqrt_fusion) | copy-start | bytes 9220
  13.1 188.0 %copy-start.22 = (f32[5120]{0:T(1024)}, f32[5120]{0:T(1024)S(1)}, u32[]{:S(2)}) copy-start(f32[5120]{0:T(1024)S(1)} %convert_element_type.146) | copy-start | bytes 61444
  25.7 62.5 %all-to-all-start.3 = ((bf16[768,8,128]{2,0,1:T(8,128)(2,1)}), bf16[768,8,128]{2,0,1:T(8,128)(2,1)S(1)}, u32[]{:S(2)}, u32[]{:S(2)}) async-start(bf16[768,8,128]{2,0,1:T(8,128)(2,1)} %bitcast.203), calls=%async_computation.3 | async-start | bytes 3145728 | tf_op jit(solution)/shard_map/all_to_all | solution.py:132
  30.5 49.1 copy-start.32
  89.4 107.8 %all-to-all-start.2 = ((bf16[768,40,128]{2,0,1:T(8,128)(2,1)}), bf16[768,40,128]{2,0,1:T(8,128)(2,1)}, u32[]{:S(2)}, u32[]{:S(2)}) async-start(bf16[768,40,128]{2,0,1:T(8,128)(2,1)} %bitcast.251), calls=%async_computation.2 | async-start | bytes 15728640 | tf_op jit(solution)/shard_map/all_to_all | solution.py:133
  93.2 49.8 copy-start.30
  158.1 56.8 %copy-start.6 = (f32[768,128]{1,0:T(8,128)}, f32[768,128]{1,0:T(8,128)S(1)}, u32[]{:S(2)}) copy-start(f32[768,128]{1,0:T(8,128)S(1)} %get-tuple-element.257) | copy-start | bytes 1179652
  158.2 56.8 %copy-start.12 = (f32[768,128]{1,0:T(8,128)}, f32[768,128]{1,0:T(8,128)S(1)}, u32[]{:S(2)}) copy-start(f32[768,128]{1,0:T(8,128)S(1)} %get-tuple-element.258) | copy-start | bytes 1179652
  158.2 24.7 slice-start.4
  158.2 24.7 slice-start.5
  158.2 24.7 slice-start.6
  158.2 24.9 slice-start.7
  197.2 92.2 %all-to-all-start = ((bf16[768,40,128]{2,0,1:T(8,128)(2,1)}), bf16[768,40,128]{2,0,1:T(8,128)(2,1)}, u32[]{:S(2)}, u32[]{:S(2)}) async-start(bf16[768,40,128]{2,0,1:T(8,128)(2,1)} %fusion.78), calls=%async_computation | async-start | bytes 15728640 | tf_op jit(solution)/shard_map/all_to_all | solution.py:130
  215.0 76.9 %copy-start.34 = (s32[3]{0:T(128)S(1)}, s32[3]{0:T(128)}, u32[]{:S(2)}) copy-start(s32[3]{0:T(128)} %param.16) | copy-start | bytes 40
  289.4 23.2 all-to-all-start.1
  291.7 4643.8 %reduce-scatter.11.cloned.1.call-start = ((), (), s32[]{:S(2)}) async-start(), calls=%async_computation.13 | async-start | bytes 23592960 | tf_op jit(solution)/shard_map/reduce_scatter | solution.py:143
  299.4 13.2 copy-start.5
  457.8 6.0 copy-start
  534.6 6.0 copy-start
  841.6 6.0 copy-start
  918.4 6.0 copy-start
  1148.7 6.0 copy-start
  1225.5 6.0 copy-start
  1532.5 6.0 copy-start
  1609.3 6.0 copy-start
  1916.4 6.0 copy-start
  4002.7 29.1 copy-start.23
  4002.7 29.1 copy-start.27
  4031.0 18.6 copy-start.9
  4031.7 17.9 copy-start.15
  4051.5 9.7 copy-start.7
  4058.8 23.2 all-to-all-start.6
  4061.2 874.4 %reduce-scatter.9.cloned.1.call-start = ((), (), s32[]{:S(2)}) async-start(), calls=%async_computation.12 | async-start | bytes 23592960 | tf_op jit(solution)/shard_map/reduce_scatter | solution.py:143
  4085.9 7.5 copy-start.13
  4097.9 7.3 copy-start.24
  4122.7 950.9 %reduce-scatter.13.cloned.1.call-start = ((), (), s32[]{:S(2)}) async-start(), calls=%async_computation.14 | async-start | bytes 117964800
  4360.8 15.7 copy-start.14
  4410.5 15.7 copy-start.17
  4493.4 1133.1 %reduce-scatter.15.cloned.1.call-start = ((), (), s32[]{:S(2)}) async-start(), calls=%async_computation.15 | async-start | bytes 117964800
  4743.3 16.2 slice-start
  4743.8 15.8 slice-start.1
  4743.8 15.8 slice-start.2
  4743.8 15.8 slice-start.3
  4743.8 15.8 copy-start.8
  4769.9 49.7 copy-start.16
  4769.9 49.7 copy-start.25
  4769.9 49.7 copy-start.28
  4819.6 25.5 copy-start.29
  (384 other events, 1246.7 us)
Sparse Core Ops, SparseCore 0:
  4049.7 188.9 reduce-scatter.10
  4242.8 151.9 reduce-scatter.8
  4493.5 580.0 reduce-scatter.12
  5077.7 548.8 reduce-scatter.14
where the time goes:
time: 5650 us; the launch traced here: 5630 us
  matrix products  2300 us (41%)
  other arithmetic  1780 us (32%)
  waiting for transfers between devices  789 us (14%)
  blocking collectives  415 us (7%)
  local copies, waits for them, and re-layouts  251 us (4%)
  loops' own time  68 us (1%)
    sub x96, other arithmetic, block_step(): d_score = (prob_f * (d_prob - row_delta) * qk_scale).astype(jnp.bfloat16)  1370 us
    unnamed x6, waiting for transfers between devices  691 us
    dot_general x96, matrix products, block_step(): jnp.einsum('gqrk,qgre->kge', d_score, q_blk, preferred_element_type=jnp.f...  573 us
    dot_general x96, matrix products, block_step(): jnp.einsum('qgre,kge->gqrk', do_blk, v_all, preferred_element_type=jnp.fl...  499 us
    dot_general x96, matrix products, block_step(): jnp.einsum('gqrk,qgre->kge', prob_b, do_blk, preferred_element_type=jnp.f...  257 us
    sub x96, other arithmetic, block_step(): prob_f = jax.nn.softmax(scores, axis=-1)  226 us
    dot_general x96, matrix products, block_step(): jnp.einsum('qgre,kge->gqrk', q_blk, k_all, preferred_element_type=jnp.flo...  208 us
    all_to_all x1, blocking collectives, per_device(): lax.all_to_all(dq_h.reshape(seq_len, loc_heads, HEAD_DIM), 'sp', 0, 1, ti...  197 us
  transfers between devices with their start and end apart: 9, of which 5 were waited for; matrix products, arithmetic and copies ran while one was open for 12% of the time, Pallas kernels for 0%

commit v1 on v0

v1 whole, which is shorter than its diff:
```python
import functools
import math
import jax
import jax.numpy as jnp
from jax import lax
from jax.experimental import pallas as pl
from jax.experimental.pallas import tpu as pltpu
from jax.sharding import PartitionSpec as P

HEAD_DIM = 128
SECTION_ONE = 16
SECTION_TWO = 40
ROPE_BASE = 1000000.0
NORM_EPS = 1e-6
LOG2E = 1.4426950408889634
NEG = -1e30
F32 = jnp.float32
BF16 = jnp.bfloat16


def rope_tables(pos_ids):
    freq_idx = jnp.arange(HEAD_DIM) % (HEAD_DIM // 2)
    exponent = 2 * freq_idx.astype(F32) / HEAD_DIM
    inv_freq = 1.0 / jnp.power(ROPE_BASE, exponent)
    pos_f = pos_ids.astype(F32)
    chosen = jnp.where(freq_idx[None, :] < SECTION_ONE, pos_f[0][:, None], jnp.where(freq_idx[None, :] < SECTION_TWO, pos_f[1][:, None], pos_f[2][:, None]))
    angles = chosen * inv_freq[None, :]
    sign = jnp.where(jnp.arange(HEAD_DIM) < HEAD_DIM // 2, -1.0, 1.0).astype(F32)
    return jnp.cos(angles), jnp.sin(angles) * sign[None, :]


def dot(a, b):
    return lax.dot_general(a, b, (((1,), (0,)), ((), ())), preferred_element_type=F32)


def dot_t(a, b):
    return lax.dot_general(a, b, (((1,), (1,)), ((), ())), preferred_element_type=F32)


def qkv_kernel(n_rot, u_ref, w_ref, b_ref, cos_ref, sin_ref, out_ref):
    lin = dot(u_ref[...], w_ref[...]) + b_ref[...]
    cos_t = cos_ref[...]
    sin_t = sin_ref[...]
    for idx in range(n_rot):
        cols = slice(idx * HEAD_DIM, (idx + 1) * HEAD_DIM)
        part = lin[:, cols]
        out_ref[:, cols] = (part * cos_t + pltpu.roll(part, HEAD_DIM // 2, 1) * sin_t).astype(BF16)
    out_ref[:, n_rot * HEAD_DIM:] = lin[:, n_rot * HEAD_DIM:].astype(BF16)


def project(u_all, w_cat, b_cat, cos_t, sin_t, n_rot):
    tokens, hidden = u_all.shape
    width = w_cat.shape[1]
    rows = math.gcd(tokens, 512)
    return pl.pallas_call(
        functools.partial(qkv_kernel, n_rot),
        out_shape=jax.ShapeDtypeStruct((tokens, width), BF16),
        grid=(tokens // rows,),
        in_specs=[
            pl.BlockSpec((rows, hidden), lambda i: (i, 0)),
            pl.BlockSpec((hidden, width), lambda i: (0, 0), pipeline_mode=pl.Buffered(1)),
            pl.BlockSpec((1, width), lambda i: (0, 0)),
            pl.BlockSpec((rows, HEAD_DIM), lambda i: (i, 0)),
            pl.BlockSpec((rows, HEAD_DIM), lambda i: (i, 0)),
        ],
        out_specs=pl.BlockSpec((rows, width), lambda i: (i, 0)),
        compiler_params=pltpu.CompilerParams(vmem_limit_bytes=60 * 1024 * 1024),
        cost_estimate=pl.CostEstimate(flops=2 * tokens * hidden * width, bytes_accessed=2 * (tokens * hidden + hidden * width + tokens * width), transcendentals=0),
        name="qkv_rope",
    )(u_all, w_cat, b_cat, cos_t, sin_t)


def attn_kernel(blk, n_heads, n_blk, cu_ref, q_ref, do_ref, k_ref, v_ref, cos_ref, sin_ref,
                o_ref, gq_ref, gk_ref, gv_ref, gbq_ref, gbk_ref, gbv_ref,
                s_scr, dp_scr, dk_scr, dv_scr, kt_scr, vt_scr):
    head = pl.program_id(0)
    row_blk = pl.program_id(1)
    half = HEAD_DIM // 2
    scale = 1.0 / math.sqrt(HEAD_DIM)
    cut = cu_ref[1]
    row_0 = row_blk * blk

    @pl.when((head == 0) & (row_blk == 0))
    def _():
        @pl.loop(0, n_blk)
        def _(c):
            rows = pl.ds(pl.multiple_of(c * blk, blk), blk)
            kt_scr[c] = k_ref[rows, :].T
            vt_scr[c] = v_ref[rows, :].T
            dk_scr[c] = jnp.zeros((blk, HEAD_DIM), F32)
            dv_scr[c] = jnp.zeros((blk, HEAD_DIM), F32)

    first_tok = jnp.where(row_0 >= cut, cut, 0)
    lo = first_tok // blk
    hi = row_blk + 1
    straddle = (row_0 < cut) & (cut < row_0 + blk)
    ragged = lo * blk < first_tok

    q_blk = q_ref[...]
    do_blk = do_ref[...]

    def scores(c, m_acc, masked):
        rows = pl.ds(pl.multiple_of(c * blk, blk), blk)
        s_t = dot_t(k_ref[rows, :], q_blk)
        if masked:
            key_idx = c * blk + lax.broadcasted_iota(jnp.int32, (blk, blk), 0)
            q_idx = row_0 + lax.broadcasted_iota(jnp.int32, (blk, blk), 1)
            start = jnp.where(q_idx >= cut, cut, 0)
            s_t = jnp.where((key_idx <= q_idx) & (key_idx >= start), s_t, NEG)
        s_scr[c] = s_t
        dp_scr[c] = dot_t(v_ref[rows, :], do_blk)
        return jnp.maximum(m_acc, jnp.max(s_t.reshape(blk // 8, 8, blk), axis=0))

    def phase_a(c, m_acc):
        need = (c == row_blk) | straddle | ((c == lo) & ragged)
        return lax.cond(need, lambda m: scores(c, m, True), lambda m: scores(c, m, False), m_acc)

    m_acc = lax.fori_loop(lo, hi, phase_a, jnp.full((8, blk), NEG, F32))
    m_row = jnp.max(m_acc, axis=0, keepdims=True) * (scale * LOG2E)

    def phase_b(c, accs):
        l_acc, d_acc = accs
        p = jnp.exp2(s_scr[c] * (scale * LOG2E) - m_row)
        s_scr[c] = p
        pd = p * dp_scr[c]
        return (l_acc + jnp.sum(p.reshape(blk // 8, 8, blk), axis=0), d_acc + jnp.sum(pd.reshape(blk // 8, 8, blk), axis=0))

    zero_8 = jnp.zeros((8, blk), F32)
    l_acc, d_acc = lax.fori_loop(lo, hi, phase_b, (zero_8, zero_8))
    inv_l = 1.0 / jnp.sum(l_acc, axis=0, keepdims=True)
    delta = jnp.sum(d_acc, axis=0, keepdims=True) * inv_l

    def phase_c(c, accs):
        o_acc, dq_acc = accs
        p = s_scr[c] * inv_l
        p_b = p.astype(BF16)
        ds_b = (p * (dp_scr[c] - delta) * scale).astype(BF16)
        o_acc = o_acc + dot(vt_scr[c], p_b)
        dq_acc = dq_acc + dot(kt_scr[c], ds_b)
        dk_scr[c] += dot(ds_b, q_blk)
        dv_scr[c] += dot(p_b, do_blk)
        return o_acc, dq_acc

    zero_t = jnp.zeros((HEAD_DIM, blk), F32)
    o_acc, dq_acc = lax.fori_loop(lo, hi, phase_c, (zero_t, zero_t))
    o_ref[...] = o_acc.T.astype(BF16)

    def unrotate(grad, rows):
        return grad * cos_ref[rows, :] + pltpu.roll(grad * sin_ref[rows, :], half, 1)

    dq = dq_acc.T.astype(BF16).astype(F32)
    gq = unrotate(dq, pl.ds(pl.multiple_of(row_0, blk), blk))
    gq_ref[...] = gq.astype(BF16)

    @pl.when(row_blk == 0)
    def _():
        gbq_ref[...] = jnp.zeros_like(gbq_ref)

    gbq_ref[...] += jnp.sum(gq.reshape(blk // 8, 8, HEAD_DIM), axis=0)

    @pl.when((head == n_heads - 1) & (row_blk == n_blk - 1))
    def _():
        gbk_ref[...] = jnp.zeros_like(gbk_ref)
        gbv_ref[...] = jnp.zeros_like(gbv_ref)

        @pl.loop(0, n_blk)
        def _(c):
            rows = pl.ds(pl.multiple_of(c * blk, blk), blk)
            gk = unrotate(dk_scr[c].astype(BF16).astype(F32), rows)
            gk_ref[rows, :] = gk.astype(BF16)
            gbk_ref[...] += jnp.sum(gk.reshape(blk // 8, 8, HEAD_DIM), axis=0)
            gv = dv_scr[c].astype(BF16)
            gv_ref[rows, :] = gv
            gbv_ref[...] += jnp.sum(gv.astype(F32).reshape(blk // 8, 8, HEAD_DIM), axis=0)


def attend(cu_doc, qkv, d_out, cos_t, sin_t, n_heads):
    tokens = qkv.shape[0]
    blk = math.gcd(tokens, 512)
    n_blk = tokens // blk
    whole = functools.partial(pl.BlockSpec, pipeline_mode=pl.Buffered(1))
    width = n_heads * HEAD_DIM
    head_blk = pl.BlockSpec((blk, HEAD_DIM), lambda h, i, cu: (i, h))
    return pl.pallas_call(
        functools.partial(attn_kernel, blk, n_heads, n_blk),
        out_shape=[
            jax.ShapeDtypeStruct((tokens, width), BF16),
            jax.ShapeDtypeStruct((tokens, width), BF16),
            jax.ShapeDtypeStruct((tokens, HEAD_DIM), BF16),
            jax.ShapeDtypeStruct((tokens, HEAD_DIM), BF16),
            jax.ShapeDtypeStruct((8, width), F32),
            jax.ShapeDtypeStruct((8, HEAD_DIM), F32),
            jax.ShapeDtypeStruct((8, HEAD_DIM), F32),
        ],
        grid_spec=pltpu.PrefetchScalarGridSpec(
            num_scalar_prefetch=1,
            grid=(n_heads, n_blk),
            in_specs=[
                head_blk,
                head_blk,
                whole((tokens, HEAD_DIM), lambda h, i, cu: (0, n_heads)),
                whole((tokens, HEAD_DIM), lambda h, i, cu: (0, n_heads + 1)),
                whole((tokens, HEAD_DIM), lambda h, i, cu: (0, 0)),
                whole((tokens, HEAD_DIM), lambda h, i, cu: (0, 0)),
            ],
            out_specs=[
                head_blk,
                head_blk,
                pl.BlockSpec((tokens, HEAD_DIM), lambda h, i, cu: (0, 0)),
                pl.BlockSpec((tokens, HEAD_DIM), lambda h, i, cu: (0, 0)),
                pl.BlockSpec((8, HEAD_DIM), lambda h, i, cu: (0, h)),
                pl.BlockSpec((8, HEAD_DIM), lambda h, i, cu: (0, 0)),
                pl.BlockSpec((8, HEAD_DIM), lambda h, i, cu: (0, 0)),
            ],
            scratch_shapes=[
                pltpu.VMEM((n_blk, blk, blk), F32),
                pltpu.VMEM((n_blk, blk, blk), F32),
                pltpu.VMEM((n_blk, blk, HEAD_DIM), F32),
                pltpu.VMEM((n_blk, blk, HEAD_DIM), F32),
                pltpu.VMEM((n_blk, HEAD_DIM, blk), BF16),
                pltpu.VMEM((n_blk, HEAD_DIM, blk), BF16),
            ],
        ),
        compiler_params=pltpu.CompilerParams(vmem_limit_bytes=63 * 1024 * 1024),
        cost_estimate=pl.CostEstimate(flops=6 * n_heads * tokens * tokens * HEAD_DIM * 2, bytes_accessed=10 * tokens * width, transcendentals=0),
        name="attn_fwd_bwd",
    )(cu_doc, qkv, d_out, qkv, qkv, cos_t, sin_t)


def solution(mesh):
    n_dev = mesh.shape["sp"]
    tok_spec = P(("dp", "sp"), None)
    vec_spec = P(("dp", "sp"))
    rep_spec = P()

    def exchange(parts):
        return lax.all_to_all(parts, "sp", 0, 0, tiled=True)

    def per_device(hidden, pos_ids, cu_doc, grad_y, norm_w, w_q, b_q, w_k, b_k, w_v, b_v, w_o):
        tokens, width = hidden.shape
        me = lax.axis_index("sp")
        q_cols = w_q.shape[1] // n_dev
        kv_cols = w_k.shape[1] // n_dev
        n_heads = q_cols // HEAD_DIM

        h_f32 = hidden.astype(F32)
        inv_rms = lax.rsqrt(jnp.mean(h_f32 * h_f32, axis=-1, keepdims=True) + NORM_EPS)
        normed = h_f32 * inv_rms
        gain = norm_w.astype(F32)
        u_loc = (normed * gain).astype(BF16)
        u_all = lax.all_gather(u_loc, "sp", axis=0, tiled=True)
        pos_all = lax.all_gather(pos_ids, "sp", axis=1, tiled=True)
        cos_t, sin_t = rope_tables(pos_all)

        d_attn = jnp.einsum("td,qd->tq", grad_y, w_o, preferred_element_type=F32).astype(BF16)
        d_parts = d_attn.reshape(tokens, n_dev, q_cols).transpose(1, 0, 2)
        d_out = exchange(d_parts).reshape(n_dev * tokens, q_cols)

        def own(w, cols):
            return lax.dynamic_slice_in_dim(w, me * cols, cols, axis=w.ndim - 1)

        w_cat = jnp.concatenate([own(w_q, q_cols), own(w_k, kv_cols), own(w_v, kv_cols)], axis=1)
        b_cat = jnp.concatenate([own(b_q, q_cols), own(b_k, kv_cols), own(b_v, kv_cols)]).astype(F32)[None, :]
        qkv = project(u_all, w_cat, b_cat, cos_t, sin_t, n_heads + kv_cols // HEAD_DIM)

        gy_src, qkv = lax.optimization_barrier((grad_y, qkv))
        gy_all = lax.all_gather(gy_src, "sp", axis=0, tiled=True)

        o_h, gq_h, gk_h, gv_h, gbq, gbk, gbv = attend(cu_doc, qkv, d_out, cos_t, sin_t, n_heads)

        o_tok = exchange(o_h.reshape(n_dev, tokens, q_cols)).transpose(1, 0, 2).reshape(tokens, n_dev * q_cols)
        gq_tok = exchange(gq_h.reshape(n_dev, tokens, q_cols)).transpose(1, 0, 2).reshape(tokens, n_dev * q_cols)
        gkv_h = jnp.stack([gk_h.reshape(n_dev, tokens, kv_cols), gv_h.reshape(n_dev, tokens, kv_cols)], axis=1)
        gkv_tok = exchange(gkv_h).transpose(1, 2, 0, 3).reshape(2, tokens, n_dev * kv_cols)

        grad_w_o = lax.dot_general(o_h, gy_all, (((0,), (0,)), ((), ())), preferred_element_type=F32)
        g_cat = jnp.concatenate([gq_h, gk_h, gv_h], axis=1)
        gw_cat = lax.dot_general(u_all, g_cat, (((0,), (0,)), ((), ())), preferred_element_type=F32)
        rows = width // n_dev
        gw_got = exchange(gw_cat.reshape(n_dev, rows, q_cols + 2 * kv_cols))

        def columns(lo, size):
            return gw_got[:, :, lo:lo + size].transpose(1, 0, 2).reshape(rows, n_dev * size)

        grad_w_q = columns(0, q_cols)
        grad_w_k = columns(q_cols, kv_cols)
        grad_w_v = columns(q_cols + kv_cols, kv_cols)

        y_out = (h_f32 + jnp.dot(o_tok, w_o, preferred_element_type=F32)).astype(BF16)
        d_norm = dot_t(gq_tok, w_q) + dot_t(gkv_tok[0], w_k) + dot_t(gkv_tok[1], w_v)
        grad_norm_w = lax.psum_scatter(jnp.sum(d_norm * normed, axis=0), "sp", scatter_dimension=0, tiled=True)
        d_scaled = d_norm * gain
        d_hidden = inv_rms * (d_scaled - normed * jnp.mean(d_scaled * normed, axis=-1, keepdims=True))
        grad_hidden = (grad_y.astype(F32) + d_hidden).astype(BF16)
        return (y_out, grad_hidden, grad_norm_w, grad_w_q, jnp.sum(gbq, axis=0), grad_w_k, jnp.sum(gbk, axis=0), grad_w_v, jnp.sum(gbv, axis=0), grad_w_o)

    in_specs = (tok_spec, P(None, ("dp", "sp")), P("dp"), tok_spec, rep_spec, rep_spec, rep_spec, rep_spec, rep_spec, rep_spec, rep_spec, rep_spec)
    out_specs = (tok_spec, tok_spec, vec_spec, tok_spec, vec_spec, tok_spec, vec_spec, tok_spec, vec_spec, tok_spec)
    return jax.shard_map(per_device, mesh=mesh, in_specs=in_specs, out_specs=out_specs, check_vma=False)
```

time: 5650 us -> 1600 us (0.28)
  matrix products: 2300 us -> 315 us
  other arithmetic: 1780 us -> 58.2 us
  waiting for transfers between devices: 789 us -> 285 us
  Pallas kernels: 0 us -> 501 us
  local copies, waits for them, and re-layouts: 251 us -> 65.4 us
  blocking collectives: 415 us -> 339 us
  loops' own time: 68 us -> 0 us
    dot_general x588 -> x7, matrix products: 2300 us -> 315 us  [the longest x3 90.3 us: dot_t(): lax.dot_general(a, b, (((1,), (1,)), ((), ())), preferred_element_type=F32)]
    sub x192 -> x0, other arithmetic: 1590 us -> none  [the longest x96 1370 us: block_step(): d_score = (prob_f * (d_prob - row_delta) * qk_scale).astype(jnp.bfloat16)]
    unnamed x6 -> x2, waiting for transfers between devices: 691 us -> 0.03 us
    pallas_call x0 -> x2, Pallas kernels: none -> 501 us  [the longest x1 427 us: attend(): pl.pallas_call(functools.partial(attn_kernel, blk, n_heads, n_blk), out_s...]
    all_to_all x3 -> x1, blocking collectives: 391 us -> 132 us  [exchange(): return lax.all_to_all(parts, 'sp', 0, 0, tiled=True)]
    all_gather x0 -> x2, waiting for transfers between devices: none -> 234 us  [the longest x1 234 us: per_device(): u_all = lax.all_gather(u_loc, 'sp', axis=0, tiled=True)]
    unnamed x1, blocking collectives: 23.6 us -> 192 us
    another operation x1 -> x0, loops' own time: 68 us -> none  [attend(): acc_pair, outs_pair = lax.scan(block_step, (zero_acc, zero_acc), blocks_in)]
  transfers between devices with their start and end apart: 9 -> 6, of which waited for: 5 -> 4; matrix products, arithmetic and copies ran while one was open for 12% -> 24% of each run, Pallas kernels for 0% -> 27%
where the time goes in v1:
time: 1600 us; the launch traced here: 1590 us
  Pallas kernels  501 us (31%)
  blocking collectives  339 us (21%)
  matrix products  315 us (20%)
  waiting for transfers between devices  285 us (18%)
  local copies, waits for them, and re-layouts  65.4 us (4%)
  other arithmetic  58.2 us (4%)
    pallas_call x1, Pallas kernels, attend(): pl.pallas_call(functools.partial(attn_kernel, blk, n_heads, n_blk), out_s...  427 us
    all_gather x1, waiting for transfers between devices, per_device(): u_all = lax.all_gather(u_loc, 'sp', axis=0, tiled=True)  234 us
    unnamed x1, blocking collectives  192 us
    all_to_all x1, blocking collectives, exchange(): return lax.all_to_all(parts, 'sp', 0, 0, tiled=True)  132 us
    dot_general x3, matrix products, dot_t(): lax.dot_general(a, b, (((1,), (1,)), ((), ())), preferred_element_type=F32)  90.3 us
    dot_general x1, matrix products, per_device(): lax.dot_general(u_all, g_cat, (((0,), (0,)), ((), ())), preferred_element...  74.8 us
    pallas_call x1, Pallas kernels, project(): pl.pallas_call(functools.partial(qkv_kernel, n_rot), out_shape=jax.ShapeD...  74.3 us
    all_to_all x4, waiting for transfers between devices, exchange(): return lax.all_to_all(parts, 'sp', 0, 0, tiled=True)  51.1 us
  transfers between devices with their start and end apart: 6, of which 4 were waited for; matrix products, arithmetic and copies ran while one was open for 24% of the time, Pallas kernels for 27%

profile of v1, /device:TPU:0, one launch (start us, length us, event | category | flops | bytes accessed | tf_op | source)
XLA Modules:
  0.0 1593.4 jit_solution(9763065401925724405)
XLA Ops:
  7.2 0.9 convert_element_type.42
  8.1 5.0 fusion.11
  13.1 6.7 fusion.4
  19.9 0.8 dynamic_slice.21
  20.7 14.1 all_gather.10
  34.8 0.8 dynamic-slice_bitcast_fusion
  35.6 0.6 maximum_convert_fusion.b_ref
  36.2 1.9 constant_dynamic-slice_fusion
  38.1 3.4 constant_dynamic-slice_fusion.2
  41.5 4.2 pad_maximum_fusion.w_ref
  45.8 22.8 %sine_multiply_fusion = (f32[6144,128]{1,0:T(8,128)}, f32[6144,128]{1,0:T(8,128)}) fusion(f32[128]{0:T(128)S(1)} %get-tuple-element.46, f32[128]{0:T(128)S(1)} %get-tuple-element.47, f32[6144]{0:T(1024)S(1)} %bitcast.76, f32[6144]{0:T(1024)S(1)} %bitcast.77, f32[6144]{0:T(1024)S(1)} %bitcast.75, pred[128]{0:T(512)(128)(4,1)S(1)} %get-tuple-element.40, ...), kind=kLoop, calls=%fused_computation.29 | loop fusion | flops 3145728 | bytes 6366464 | tf_op jit(solution)/shard_map/mul | solution.py:29
  68.6 233.7 %all-gather.3.cloned.1.call-done.u_ref = bf16[6144,5120]{1,0:T(8,128)(2,1)} async-done(((bf16[768,5120]{1,0:T(8,128)(2,1)}), bf16[6144,5120]{1,0:T(8,128)(2,1)}) %all-gather.3.cloned.1.call-update) | async-done | bytes 62914576 | tf_op jit(solution)/shard_map/all_gather | solution.py:251
  302.3 74.3 %qkv_rope.1.q_ref.k_ref.v_ref = bf16[6144,896]{1,0:T(8,128)(2,1)} custom-call(bf16[6144,5120]{1,0:T(8,128)(2,1)} %all-gather.3.cloned.1.call-done.u_ref, bf16[5120,896]{1,0:T(8,128)(2,1)} %pad_maximum_fusion.w_ref, f32[1,896]{1,0:T(1,128)} %maximum_convert_fusion.b_ref, f32[6144,128]{1,0:T(8,128)} %get-tuple-element.38.cos_ref, ...), custom_call_target="tpu_custom_call" | custom-call | flops 56371445760 | bytes 83099648 | tf_op jit(solution)/shard_map/qkv_rope/pallas_call | solution.py:55
  376.6 49.3 %convolution_convert_fusion = bf16[768,5120]{1,0:T(8,128)(2,1)} fusion(bf16[768,5120]{1,0:T(8,128)(2,1)} %param.15, bf16[5120,5120]{1,0:T(8,128)(2,1)} %param.23), kind=kOutput, calls=%fused_computation.25 | convolution fusion | flops 40269250560 | bytes 68157440 | tf_op jit(solution)/shard_map/td,qd->tq/dot_general | solution.py:255
  425.9 4.0 copy.51
  429.9 132.3 %all_to_all.25 = bf16[8,768,640]{2,1,0:T(8,128)(2,1)} all-to-all(bf16[8,768,640]{2,1,0:T(8,128)(2,1)S(1)} %bitcast.61), channel_id=1, replica_groups=mesh['dp'=1,'sp'=8] {'sp'}, dimensions={0} | all-to-all | bytes 15728640 | tf_op jit(solution)/shard_map/all_to_all | solution.py:237
  562.2 427.0 %attn_fwd_bwd.1 = (bf16[6144,640]{1,0:T(8,128)(2,1)}, bf16[6144,640]{1,0:T(8,128)(2,1)}, bf16[6144,128]{1,0:T(8,128)(2,1)}, bf16[6144,128]{1,0:T(8,128)(2,1)}, f...) custom-call(s32[3]{0:T(128)} %cu_ref.1, bf16[6144,896]{1,0:T(8,128)(2,1)} %qkv_rope.1.q_ref.k_ref.v_ref, ...), custom_call_target="tpu_custom_call" | custom-call | flops 289910292480 | bytes 39321600 | tf_op jit(solution)/shard_map/attn_fwd_bwd/pallas_call | solution.py:184
  989.2 1.7 copy.37
  990.9 1.7 copy.38
  992.6 2.0 pad_maximum_fusion.1
  994.6 2.4 all-to-all-start.3
  997.0 10.6 copy.36
  1007.6 27.2 %all-to-all-done.3 = bf16[8,2,768,128]{2,3,1,0:T(8,128)(2,1)S(1)} async-done(((bf16[8,2,768,128]{2,3,1,0:T(8,128)(2,1)}), bf16[8,2,768,128]{2,3,1,0:T(8,128)(2,1)S(1)}, u32[]{:S(2)}, u32[]{:S(2)}) %all-to-all-start.3) | async-done | bytes 3145760 | tf_op jit(solution)/shard_map/all_to_all | solution.py:237
  1034.8 4.1 all-to-all-start.2
  1039.0 10.6 copy.35
  1049.6 0.6 reduce_sum.57
  1050.2 0.5 reduce_sum.58
  1050.7 0.5 reduce_sum.59
  1051.2 74.8 %fusion.13 = f32[5120,896]{1,0:T(8,128)} fusion(bf16[6144,5120]{1,0:T(8,128)(2,1)} %all-gather.3.cloned.1.call-done.u_ref, bf16[6144,128]{1,0:T(8,128)(2,1)} %get-tuple-element.23, bf16[6144,128]{1,0:T(8,128)(2,1)} %get-tuple-element.22, bf16[6144,640]{1,0:T(8,128)(2,1)} %get-tuple-element.21), kind=kOutput, calls=%fused_computation.18 | convolution fusion | flops 56404475904 | bytes 92274688 | tf_op jit(solution)/shard_map/dot_general | solution.py:278
  1126.1 0.2 copy.52
  1126.3 0.2 fusion.21
  1126.5 0.8 all-to-all-done.2
  1127.3 3.8 all-to-all-start.1
  1131.1 15.5 fusion.24
  1146.6 49.7 %fusion.23 = f32[768,5120]{1,0:T(8,128)} fusion(bf16[768,5120]{0,1:T(8,128)(2,1)} %bitcast.12, bf16[5120,5120]{1,0:T(8,128)(2,1)} %param.17), kind=kOutput, calls=%fused_computation.52 | convolution fusion | flops 40265318400 | bytes 76021760 | tf_op jit(solution)/shard_map/dot_general | solution.py:37
  1196.3 23.2 %all-to-all-done.1 = bf16[8,768,640]{1,2,0:T(8,128)(2,1)} async-done(((bf16[8,768,640]{1,2,0:T(8,128)(2,1)}), bf16[8,768,640]{1,2,0:T(8,128)(2,1)}, u32[]{:S(2)}, u32[]{:S(2)}) %all-to-all-start.1) | async-done | bytes 7864352 | tf_op jit(solution)/shard_map/all_to_all | solution.py:237
  1219.5 4.9 all-to-all-start.4
  1224.4 25.2 %fusion.10 = (f32[5120]{0:T(1024)S(1)}, f32[768]{0:T(1024)S(1)}, f32[768,5120]{1,0:T(8,128)}) fusion(bf16[768,5120]{1,0:T(8,128)(2,1)} %param.12, f32[768]{0:T(1024)S(1)} %copy-done.4, f32[5120]{0:T(1024)S(1)} %copy-done.2, bf16[768,1024]{0,1:T(8,128)(2,1)S(1)} %bitcast.69, bf16[5120,1024]{1,0:T(8,128)(2,1)} %param.21, f32[768,5120]{1,0:T(8,128)} %fusion.23, ...), kind=kOutput, calls=%fused_computation.13 | convolution fusion | flops 8088446976 | bytes 67155968 | tf_op jit(solution)/shard_map/dot_general | solution.py:37
  1249.6 192.3 %all-reduce = f32[5120]{0:T(1024)S(1)} all-reduce(f32[5120]{0:T(1024)S(1)} %get-tuple-element.28), channel_id=2, replica_groups=mesh['dp'=1,'sp'=8] {'sp'}, use_global_device_ids=true, to_apply=%region_3.4.clone | all-reduce | flops 5120 | bytes 40960
  1441.9 0.7 dynamic-slice
  1442.5 14.4 fusion.9
  1457.0 50.0 %fusion.12 = bf16[768,5120]{1,0:T(8,128)(2,1)} fusion(bf16[768,5120]{1,0:T(8,128)(2,1)} %param.12, bf16[768,5120]{0,1:T(8,128)(2,1)} %bitcast.9, bf16[5120,5120]{1,0:T(8,128)(2,1)} %param.23), kind=kOutput, calls=%fused_computation.15 | convolution fusion | flops 40277114880 | bytes 76021760 | tf_op jit(solution)/shard_map/dot_general | solution.py:289
  1507.0 10.6 slice_bitcast_fusion
  1517.6 11.5 copy.44
  1529.1 2.9 slice_bitcast_fusion.1
  1532.0 1.8 copy.53
  1533.9 1.8 copy.54
  1535.7 50.4 %fusion.25 = f32[640,5120]{1,0:T(8,128)} fusion(bf16[6144,640]{1,0:T(8,128)(2,1)} %get-tuple-element.20, bf16[6144,5120]{1,0:T(8,128)(2,1)} %all-gather.5.cloned.1.call-done), kind=kOutput, calls=%fused_computation.54 | convolution fusion | flops 40265318400 | bytes 83886080 | tf_op jit(solution)/shard_map/dot_general | solution.py:276
  (31 shorter events, 0.3 us)
Async XLA Ops:
  7.2 295.1 %all-gather.3.cloned.1.call-start = ((), (), s32[]{:S(2)}) async-start(), calls=%async_computation.5 | async-start | bytes 70778880 | tf_op jit(solution)/shard_map/all_gather | solution.py:251
  7.2 5.9 copy-start
  8.1 11.7 copy-start.1
  13.1 6.8 copy-start.3
  13.1 7.6 copy-start.6
  19.9 1515.8 %all-gather.5.cloned.1.call-start = ((), (), s32[]{:S(2)}) async-start(), calls=%async_computation.6 | async-start | bytes 70778880 | tf_op jit(solution)/shard_map/all_gather | solution.py:267
  994.6 40.2 %all-to-all-start.3 = ((bf16[8,2,768,128]{2,3,1,0:T(8,128)(2,1)}), bf16[8,2,768,128]{2,3,1,0:T(8,128)(2,1)S(1)}, u32[]{:S(2)}, u32[]{:S(2)}) async-start(bf16[8,2,768,128]{2,3,1,0:T(8,128)(2,1)} %pad_maximum_fusion.1), calls=%async_computation.3 | async-start | bytes 6291456 | tf_op jit(solution)/shard_map/all_to_all | solution.py:237
  1034.8 92.5 %all-to-all-start.2 = ((bf16[8,768,640]{1,2,0:T(8,128)(2,1)}), bf16[8,768,640]{1,2,0:T(8,128)(2,1)}, u32[]{:S(2)}, u32[]{:S(2)}) async-start(bf16[8,768,640]{1,2,0:T(8,128)(2,1)} %copy.36), calls=%async_computation.2 | async-start | bytes 15728640 | tf_op jit(solution)/shard_map/all_to_all | solution.py:237
  1038.9 10.7 copy-start.5
  1038.9 11.2 copy-start.8
  1038.9 11.8 copy-start.7
  1127.3 92.2 %all-to-all-start.1 = ((bf16[8,768,640]{1,2,0:T(8,128)(2,1)}), bf16[8,768,640]{1,2,0:T(8,128)(2,1)}, u32[]{:S(2)}, u32[]{:S(2)}) async-start(bf16[8,768,640]{1,2,0:T(8,128)(2,1)} %copy.35), calls=%async_computation.1 | async-start | bytes 15728640 | tf_op jit(solution)/shard_map/all_to_all | solution.py:237
  1219.5 4.9 copy-start.2
  1219.5 4.9 copy-start.4
  1219.5 287.5 %all-to-all-start.4 = ((f32[8,640,896]{2,1,0:T(8,128)}), f32[8,640,896]{2,1,0:T(8,128)}, u32[]{:S(2)}, u32[]{:S(2)}) async-start(f32[8,640,896]{2,1,0:T(8,128)} %bitcast.62), calls=%async_computation.4 | async-start | bytes 36700160 | tf_op jit(solution)/shard_map/all_to_all | solution.py:237
Sparse Core Ops, SparseCore 0:
  20.0 282.2 all-gather.2
  376.8 363.7 all-gather.4
